TPU v7x, 32 devices: a whole 2x2x4 slice. The times are simulated.
32 devices in a mesh: rows: 8 (over z, y), groups: 4 (over x, core).
Axes of the slice: x: 2, y: 2, z: 4, core: 2. Of those that a mesh axis runs over, the one named last changes fastest.
Arguments:
- basis: bfloat16 [8, 131072, 128], P(None, ('rows', 'groups')), may hold values from -6 to 6
- image: bfloat16 [8, 131072, 128], P(None, ('rows', 'groups')), may hold values from -6 to 6
- selection: int32 [8, 64], replicated, may hold values from 0 to 127, all different within a row
Outputs:
- rotated: bfloat16 [8, 131072, 128], P(None, ('rows', 'groups'))
Inputs may be any that keep to these rules, and one draw needn't show every extreme that they name: Each row of selection names 64 different columns.
All inputs are finite; a program needn't handle non-finite values.
Results may differ from a plain program's by a relative error of at most 0.005.
Values may be sent and summed in bfloat16 or wider, within the bound.
A program may use at most 128 MiB of HBM per device.

v0:
```python
import jax
import jax.numpy as jnp
from jax import lax
from jax.sharding import PartitionSpec as P

ITERS = 3


def small_solve(grams, chosen, total_rows):
    gram_s, cross, gram_f = (grams[0], grams[1], grams[2])
    width = gram_s.shape[0]
    coeffs = (jnp.arange(width, dtype=jnp.int32)[:, None] == chosen[None, :]).astype(jnp.float32)
    factor = jnp.linalg.cholesky(gram_f)
    for step in range(ITERS):
        moved = jnp.dot(cross.T, coeffs, precision=lax.Precision.HIGHEST)
        halfway = lax.linalg.triangular_solve(factor, moved, left_side=True, lower=True)
        solved = lax.linalg.triangular_solve(
            factor, halfway, left_side=True, lower=True, transpose_a=True
        )
        metric = (
            jnp.dot(
                solved.T,
                jnp.dot(gram_s, solved, precision=lax.Precision.HIGHEST),
                precision=lax.Precision.HIGHEST,
            )
            / total_rows
        )
        lower = jnp.linalg.cholesky(metric)
        coeffs = lax.linalg.triangular_solve(
            lower, solved, left_side=False, lower=True, transpose_a=True
        )
    return coeffs


def on_device(basis, image, selection):
    total_rows = basis.shape[1] * lax.axis_size("rows") * lax.axis_size("groups")
    gram_s = jnp.einsum("srk,srl->skl", basis, basis, preferred_element_type=jnp.float32)
    cross = jnp.einsum("srk,srl->skl", basis, image, preferred_element_type=jnp.float32)
    gram_f = jnp.einsum("srk,srl->skl", image, image, preferred_element_type=jnp.float32)
    partial_grams = jnp.stack([gram_s, cross, gram_f], axis=1)
    solver = jax.vmap(lambda grams, chosen: small_solve(grams, chosen, total_rows))
    shares = lax.psum_scatter(partial_grams, "groups", scatter_dimension=0, tiled=True)
    summed = lax.psum(shares, "rows")
    grams = summed
    count = shares.shape[0]
    start = lax.axis_index("groups") * count
    mine = lax.dynamic_slice_in_dim(selection, start, count, 0)
    local_coeffs = solver(grams, mine).astype(jnp.bfloat16)
    narrow = lax.all_gather(local_coeffs, "groups", axis=0, tiled=True)
    first = jnp.einsum("srk,skj->srj", basis, narrow, preferred_element_type=jnp.float32)
    second = jnp.einsum("srk,skj->srj", image, narrow, preferred_element_type=jnp.float32)
    return jnp.concatenate([first, second], axis=2).astype(jnp.bfloat16)


def solution(mesh):
    in_specs = (P(None, ("rows", "groups"), None), P(None, ("rows", "groups"), None), P())
    out_specs = P(None, ("rows", "groups"), None)
    return jax.shard_map(
        on_device, mesh=mesh, in_specs=in_specs, out_specs=out_specs, check_vma=False
    )
```

profile of v0, /device:TPU:0, one launch (start us, length us, event | category | flops | bytes accessed | tf_op | source)
XLA Modules:
  0.0 317.1 jit_solution(13355528183286181943)
XLA Ops:
  6.5 0.0 copy-start
  6.5 0.0 all-reduce.6.cloned.1.call-start
  6.5 0.0 copy-start.1
  6.5 8.5 %convolution_bitcast_fusion.2 = f32[8,1,128,128]{3,2,0,1:T(8,128)S(1)} fusion(bf16[8,4096,128]{2,1,0:T(8,128)(2,1)} %param.10), kind=kOutput, calls=%fused_computation.8 | convolution fusion | flops 1073741824 | bytes 8912896 | tf_op jit(solution)/shard_map/srk,srl->skl/dot_general | solution.py:37
  15.0 0.0 copy-done.1
  15.0 5.9 %convolution_bitcast_fusion.1 = f32[8,1,128,128]{3,2,0,1:T(8,128)S(1)} fusion(bf16[8,4096,128]{2,1,0:T(8,128)(2,1)} %param.10, bf16[8,4096,128]{2,1,0:T(8,128)(2,1)S(1)} %copy-done.1), kind=kOutput, calls=%fused_computation.7 | convolution fusion | flops 1073741824 | bytes 17301504 | tf_op jit(solution)/shard_map/srk,srl->skl/dot_general | solution.py:38
  21.0 0.0 copy-start.2
  21.0 2.6 convolution_bitcast_fusion
  23.6 0.1 pad_maximum_fusion.1
  23.7 1.6 copy.51
  25.3 0.0 all-reduce.6.cloned.1.call-update
  25.4 0.2 all-reduce.4.cloned.1.call-start
  25.6 0.0 copy-done.2
  25.6 0.6 dynamic-slice
  26.9 44.3 %all-reduce.6.cloned.1.call-done = f32[8,3,128,128]{2,3,0,1:T(8,128)} async-done(((f32[8,3,128,128]{2,3,0,1:T(8,128)}), f32[8,3,128,128]{2,3,0,1:T(8,128)}) %all-reduce.6.cloned.1.call-update) | async-done | bytes 1572880
  71.1 1.8 constant_dynamic-slice_fusion
  72.9 0.0 all-reduce.4.cloned.1.call-update
  72.9 0.0 copy-done
  73.0 73.3 %all-reduce.4.cloned.1.call-done = f32[2,3,128,128]{2,3,0,1:T(8,128)} async-done(((f32[2,3,128,128]{2,3,0,1:T(8,128)}), f32[2,3,128,128]{2,3,0,1:T(8,128)}) %all-reduce.4.cloned.1.call-update) | async-done | bytes 393232 | tf_op jit(solution)/shard_map/psum | solution.py:43
  146.3 0.9 slice_bitcast_fusion.2
  147.2 0.1 copy.52
  147.3 0.9 fusion.3
  148.3 23.5 %custom-call.16 = f32[2,128,128]{2,1,0:T(8,128)S(1)} custom-call(f32[2,128,128]{2,1,0:T(8,128)S(1)} %fusion.3), custom_call_target="Cholesky" | custom-call | tf_op jit(solution)/shard_map/vmap(jit(cholesky))/cholesky | solution.py:13
  171.8 0.1 compare_reduce_fusion.3
  171.9 0.1 select_bitcast_fusion
  172.0 19.7 %custom-call.34 = f32[2,1,128,128]{2,3,1,0:T(8,128)S(1)} custom-call(f32[2,1,128,128]{3,2,1,0:T(8,128)S(1)} %select_bitcast_fusion), custom_call_target="InvertDiagBlocksLowerTriangular" | custom-call | tf_op jit(solution)/shard_map/vmap()/triangular_solve/custom-call.3 | solution.py:17
  191.7 1.2 fusion.18
  192.8 0.2 fusion.4
  193.1 0.4 fusion.6
  193.5 1.2 fusion.21
  194.6 0.2 convolution_multiply_fusion.2
  194.9 0.1 copy.63
  195.0 11.7 %custom-call.27 = f32[2,64,64]{2,1,0:T(8,128)S(1)} custom-call(f32[2,64,64]{2,1,0:T(8,128)S(1)} %fusion.27), custom_call_target="Cholesky" | custom-call | tf_op jit(solution)/shard_map/vmap(jit(cholesky))/cholesky | solution.py:28
  206.7 0.1 compare_reduce_fusion.2
  206.8 0.1 select_bitcast_fusion.3
  206.9 9.8 %custom-call.28 = f32[2,1,64,64]{2,3,1,0:T(8,128)S(1)} custom-call(f32[2,1,64,64]{3,2,1,0:T(8,128)S(1)} %select_bitcast_fusion.3), custom_call_target="InvertDiagBlocksLowerTriangular" | custom-call | tf_op jit(solution)/shard_map/vmap()/triangular_solve/custom-call.4 | solution.py:29
  216.8 0.3 convolution_bitcast_fusion.5
  217.1 1.3 fusion.17
  218.3 0.2 fusion.8
  218.6 0.4 fusion.10
  219.0 1.2 fusion.20
  220.1 0.2 convolution_multiply_fusion.1
  220.4 0.1 copy.70
  220.5 11.7 %custom-call.31 = f32[2,64,64]{2,1,0:T(8,128)S(1)} custom-call(f32[2,64,64]{2,1,0:T(8,128)S(1)} %fusion.25), custom_call_target="Cholesky" | custom-call | tf_op jit(solution)/shard_map/vmap(jit(cholesky))/cholesky | solution.py:28
  232.2 0.1 compare_reduce_fusion.1
  232.4 0.1 select_bitcast_fusion.2
  232.4 10.0 %custom-call.32 = f32[2,1,64,64]{2,3,1,0:T(8,128)S(1)} custom-call(f32[2,1,64,64]{3,2,1,0:T(8,128)S(1)} %select_bitcast_fusion.2), custom_call_target="InvertDiagBlocksLowerTriangular" | custom-call | tf_op jit(solution)/shard_map/vmap()/triangular_solve/custom-call.4 | solution.py:29
  242.5 0.3 convolution_bitcast_fusion.4
  242.8 1.3 fusion.16
  244.1 0.2 fusion.12
  244.3 0.4 fusion.14
  244.7 1.2 fusion.19
  245.8 0.2 convolution_multiply_fusion
  246.1 0.1 copy.77
  246.2 11.7 %custom-call.35 = f32[2,64,64]{2,1,0:T(8,128)S(1)} custom-call(f32[2,64,64]{2,1,0:T(8,128)S(1)} %fusion.23), custom_call_target="Cholesky" | custom-call | tf_op jit(solution)/shard_map/vmap(jit(cholesky))/cholesky | solution.py:28
  257.9 0.1 compare_reduce_fusion
  258.1 0.1 select_bitcast_fusion.1
  258.1 9.8 %custom-call.36 = f32[2,1,64,64]{2,3,1,0:T(8,128)S(1)} custom-call(f32[2,1,64,64]{3,2,1,0:T(8,128)S(1)} %select_bitcast_fusion.1), custom_call_target="InvertDiagBlocksLowerTriangular" | custom-call | tf_op jit(solution)/shard_map/vmap()/triangular_solve/custom-call.4 | solution.py:29
  268.0 0.3 fusion.2
  268.3 5.4 %all_gather.3 = bf16[8,128,64]{1,2,0:T(8,128)(2,1)S(1)} all-gather(bf16[2,128,64]{1,2,0:T(8,128)(2,1)S(1)} %fusion.2), channel_id=1, replica_groups=mesh['rows'=8,'groups'=4] {'groups'}, dimensions={0}, use_global_device_ids=true | all-gather | bytes 163840 | tf_op jit(solution)/shard_map/all_gather | solution.py:49
  273.7 8.4 %fusion.1 = bf16[8,4096,64]{1,2,0:T(8,128)(2,1)} fusion(bf16[8,128,64]{1,2,0:T(8,128)(2,1)S(1)} %all_gather.3, bf16[8,4096,128]{2,1,0:T(8,128)(2,1)} %param.11), kind=kOutput, calls=%fused_computation.4 | convolution fusion | flops 538968064 | bytes 12713984 | tf_op jit(solution)/shard_map/srk,skj->srj/dot_general | solution.py:51
  282.1 8.4 %fusion = bf16[8,4096,64]{1,2,0:T(8,128)(2,1)} fusion(bf16[8,128,64]{1,2,0:T(8,128)(2,1)S(1)} %all_gather.3, bf16[8,4096,128]{2,1,0:T(8,128)(2,1)} %param.10), kind=kOutput, calls=%fused_computation.3 | convolution fusion | flops 538968064 | bytes 12713984 | tf_op jit(solution)/shard_map/srk,skj->srj/dot_general | solution.py:50
  290.5 7.8 %pad_maximum_fusion = bf16[8,4096,128]{1,2,0:T(8,128)(2,1)} fusion(bf16[8,4096,64]{1,2,0:T(8,128)(2,1)} %fusion.1, bf16[8,4096,64]{1,2,0:T(8,128)(2,1)} %fusion), kind=kLoop, calls=%fused_computation | loop fusion | flops 16777216 | bytes 16777216 | tf_op jit(solution)/shard_map/concatenate | solution.py:52
  298.3 11.9 %copy.79 = bf16[8,4096,128]{2,1,0:T(8,128)(2,1)} copy(bf16[8,4096,128]{1,2,0:T(8,128)(2,1)} %pad_maximum_fusion) | data formatting | bytes 16777216 | tf_op jit(solution)/shard_map/concatenate | solution.py:52
  (12 shorter events, 0.2 us)
Async XLA Ops:
  6.5 66.4 %copy-start = (s32[8,64]{1,0:T(8,128)S(1)}, s32[8,64]{1,0:T(8,128)}, u32[]{:S(2)}) copy-start(s32[8,64]{1,0:T(8,128)} %param.12) | copy-start | bytes 6148
  6.5 64.6 %all-reduce.6.cloned.1.call-start = ((), (), s32[]{:S(2)}) async-start(), calls=%async_computation.1 | async-start | bytes 3145728
  6.5 8.5 %copy-start.1 = (bf16[8,4096,128]{2,1,0:T(8,128)(2,1)S(1)}, bf16[8,4096,128]{2,1,0:T(8,128)(2,1)}, u32[]{:S(2)}) copy-start(bf16[8,4096,128]{2,1,0:T(8,128)(2,1)} %param.11) | copy-start | bytes 25165828
  21.0 4.6 %copy-start.2 = (u32[32]{0:T(128)S(1)}, u32[32]{0:T(128)}, u32[]{:S(2)}) copy-start(u32[32]{0:T(128)} %constant.92) | copy-start | bytes 388
  25.4 120.9 %all-reduce.4.cloned.1.call-start = ((), (), s32[]{:S(2)}) async-start(), calls=%async_computation | async-start | bytes 786432 | tf_op jit(solution)/shard_map/psum | solution.py:43
Sparse Core Ops, SparseCore 0:
  25.5 45.6 all-reduce.5
  74.5 71.7 all-reduce.3
where the time goes:
time: 318 us; the launch traced here: 317 us
  other arithmetic  118 us (37%)
  waiting for transfers between devices  118 us (37%)
  matrix products  44.3 us (14%)
  local copies, waits for them, and re-layouts  17.2 us (5%)
  between operations  14.4 us (5%)
  blocking collectives  5.42 us (2%)
    psum x1, waiting for transfers between devices, on_device(): summed = lax.psum(shares, 'rows')  73.3 us
    unnamed x3, waiting for transfers between devices  44.3 us
    another operation x10, other arithmetic, small_solve(): lower = jnp.linalg.cholesky(metric)  35.6 us
    another operation x7, other arithmetic, small_solve(): lax.linalg.triangular_solve(lower, solved, left_side=False, lower=True, t...  30 us
    another operation x4, other arithmetic, small_solve(): factor = jnp.linalg.cholesky(gram_f)  23.6 us
    another operation x3, other arithmetic, small_solve(): lax.linalg.triangular_solve(factor, halfway, left_side=True, lower=True,...  19.8 us
    concatenate x1, local copies, waits for them, and re-layouts, on_device(): return jnp.concatenate([first, second], axis=2).astype(jnp.bfloat16)  11.9 us
    dot_general x1, matrix products, on_device(): jnp.einsum('srk,srl->skl', basis, basis, preferred_element_type=jnp.float32)  8.47 us
  transfers between devices with their start and end apart: 2, of which 2 were waited for; matrix products, arithmetic and copies ran while one was open for 0% of the time, Pallas kernels for 0%

commit v1 on v0

--- a/solution.py
+++ b/solution.py
@@ -40,7 +40,7 @@
     partial_grams = jnp.stack([gram_s, cross, gram_f], axis=1)
     solver = jax.vmap(lambda grams, chosen: small_solve(grams, chosen, total_rows))
     shares = lax.psum_scatter(partial_grams, "groups", scatter_dimension=0, tiled=True)
-    summed = lax.psum(shares, "rows")
+    summed = jnp.sum(lax.all_gather(shares, "rows"), axis=0)
     grams = summed
     count = shares.shape[0]
     start = lax.axis_index("groups") * count

time: 318 us -> 299 us (0.940)
  waiting for transfers between devices: 118 us -> 105 us
  matrix products: 44.3 us -> 38.7 us
    psum x1 -> x0, waiting for transfers between devices: 73.3 us -> none  [on_device(): summed = lax.psum(shares, 'rows')]
    all_gather x0 -> x1, waiting for transfers between devices: none -> 60.4 us  [on_device(): summed = jnp.sum(lax.all_gather(shares, 'rows'), axis=0)]
where the time goes in v1:
time: 299 us; the launch traced here: 298 us
  other arithmetic  120 us (40%)
  waiting for transfers between devices  105 us (35%)
  matrix products  38.7 us (13%)
  local copies, waits for them, and re-layouts  14.7 us (5%)
  between operations  14.4 us (5%)
  blocking collectives  5.42 us (2%)
    all_gather x1, waiting for transfers between devices, on_device(): summed = jnp.sum(lax.all_gather(shares, 'rows'), axis=0)  60.4 us
    unnamed x3, waiting for transfers between devices  44.3 us
    another operation x10, other arithmetic, small_solve(): lower = jnp.linalg.cholesky(metric)  35.6 us
    another operation x7, other arithmetic, small_solve(): lax.linalg.triangular_solve(lower, solved, left_side=False, lower=True, t...  30 us
    another operation x4, other arithmetic, small_solve(): factor = jnp.linalg.cholesky(gram_f)  23.6 us
    another operation x3, other arithmetic, small_solve(): lax.linalg.triangular_solve(factor, halfway, left_side=True, lower=True,...  19.8 us
    concatenate x1, local copies, waits for them, and re-layouts, on_device(): return jnp.concatenate([first, second], axis=2).astype(jnp.bfloat16)  11.9 us
    dot_general x1, matrix products, on_device(): jnp.einsum('srk,skj->srj', image, narrow, preferred_element_type=jnp.floa...  8.41 us
  transfers between devices with their start and end apart: 2, of which 2 were waited for; matrix products, arithmetic and copies ran while one was open for 0% of the time, Pallas kernels for 0%

profile of v1, /device:TPU:0, one launch (start us, length us, event | category | flops | bytes accessed | tf_op | source)
XLA Modules:
  0.0 298.4 jit_solution(9046712516652795404)
XLA Ops:
  6.5 0.0 copy-start
  6.5 0.0 all-reduce.3.cloned.1.call-start
  6.5 0.0 copy-start.1
  6.5 8.4 %convolution_bitcast_fusion.2 = f32[8,1,128,128]{3,2,0,1:T(8,128)S(1)} fusion(bf16[8,4096,128]{2,1,0:T(8,128)(2,1)} %param.10), kind=kOutput, calls=%fused_computation.8 | convolution fusion | flops 1073741824 | bytes 8912896 | tf_op jit(solution)/shard_map/srk,srl->skl/dot_general | solution.py:37
  14.9 0.0 copy-done.1
  15.0 5.9 %convolution_bitcast_fusion.1 = f32[8,1,128,128]{3,2,0,1:T(8,128)S(1)} fusion(bf16[8,4096,128]{2,1,0:T(8,128)(2,1)} %param.10, bf16[8,4096,128]{2,1,0:T(8,128)(2,1)S(1)} %copy-done.1), kind=kOutput, calls=%fused_computation.7 | convolution fusion | flops 1073741824 | bytes 17301504 | tf_op jit(solution)/shard_map/srk,srl->skl/dot_general | solution.py:38
  20.8 0.0 copy-start.2
  20.8 2.5 convolution_bitcast_fusion
  23.3 1.2 pad_maximum_fusion.1
  24.6 0.0 all-reduce.3.cloned.1.call-update
  24.6 0.2 all-gather.3.cloned.1.call-start
  24.8 0.0 copy-done.2
  24.8 0.6 dynamic-slice
  26.1 44.3 %all-reduce.3.cloned.1.call-done = f32[8,3,128,128]{3,2,0,1:T(8,128)} async-done(((f32[8,3,128,128]{3,2,0,1:T(8,128)}), f32[8,3,128,128]{3,2,0,1:T(8,128)}) %all-reduce.3.cloned.1.call-update) | async-done | bytes 1572880
  70.4 1.8 constant_dynamic-slice_fusion
  72.1 0.0 all-gather.3.cloned.1.call-update
  72.2 0.0 copy-done
  72.3 60.4 %all-gather.3.cloned.1.call-done = f32[16,3,128,128]{3,2,0,1:T(8,128)} async-done(((f32[2,3,128,128]{3,2,0,1:T(8,128)}), f32[16,3,128,128]{3,2,0,1:T(8,128)}) %all-gather.3.cloned.1.call-update) | async-done | bytes 3145744 | tf_op jit(solution)/shard_map/all_gather | solution.py:43
  132.7 2.1 reduce_sum.9
  134.8 0.2 fusion.18
  135.0 0.1 copy.88
  135.2 23.5 %custom-call.16 = f32[2,128,128]{2,1,0:T(8,128)S(1)} custom-call(f32[2,128,128]{2,1,0:T(8,128)S(1)} %fusion.3), custom_call_target="Cholesky" | custom-call | tf_op jit(solution)/shard_map/vmap(jit(cholesky))/cholesky | solution.py:13
  158.7 0.1 compare_reduce_fusion.3
  158.8 0.1 select_bitcast_fusion
  158.9 19.7 %custom-call.34 = f32[2,1,128,128]{2,3,1,0:T(8,128)S(1)} custom-call(f32[2,1,128,128]{3,2,1,0:T(8,128)S(1)} %select_bitcast_fusion), custom_call_target="InvertDiagBlocksLowerTriangular" | custom-call | tf_op jit(solution)/shard_map/vmap()/triangular_solve/custom-call.3 | solution.py:17
  178.6 0.2 fusion.4
  178.8 0.4 fusion.6
  179.2 0.4 fusion.21
  179.5 0.2 convolution_multiply_fusion.2
  179.8 0.1 copy.58
  179.9 11.7 %custom-call.27 = f32[2,64,64]{2,1,0:T(8,128)S(1)} custom-call(f32[2,64,64]{2,1,0:T(8,128)S(1)} %fusion.27), custom_call_target="Cholesky" | custom-call | tf_op jit(solution)/shard_map/vmap(jit(cholesky))/cholesky | solution.py:28
  191.7 0.1 compare_reduce_fusion.2
  191.8 0.1 select_bitcast_fusion.3
  191.9 9.8 %custom-call.28 = f32[2,1,64,64]{2,3,1,0:T(8,128)S(1)} custom-call(f32[2,1,64,64]{3,2,1,0:T(8,128)S(1)} %select_bitcast_fusion.3), custom_call_target="InvertDiagBlocksLowerTriangular" | custom-call | tf_op jit(solution)/shard_map/vmap()/triangular_solve/custom-call.4 | solution.py:29
  201.7 0.3 convolution_bitcast_fusion.5
  202.0 0.2 fusion.17
  202.3 0.2 fusion.8
  202.5 0.4 fusion.10
  202.9 0.4 fusion.20
  203.2 0.2 convolution_multiply_fusion.1
  203.5 0.1 copy.63
  203.6 11.7 %custom-call.31 = f32[2,64,64]{2,1,0:T(8,128)S(1)} custom-call(f32[2,64,64]{2,1,0:T(8,128)S(1)} %fusion.25), custom_call_target="Cholesky" | custom-call | tf_op jit(solution)/shard_map/vmap(jit(cholesky))/cholesky | solution.py:28
  215.4 0.1 compare_reduce_fusion.1
  215.5 0.1 select_bitcast_fusion.2
  215.6 10.0 %custom-call.32 = f32[2,1,64,64]{2,3,1,0:T(8,128)S(1)} custom-call(f32[2,1,64,64]{3,2,1,0:T(8,128)S(1)} %select_bitcast_fusion.2), custom_call_target="InvertDiagBlocksLowerTriangular" | custom-call | tf_op jit(solution)/shard_map/vmap()/triangular_solve/custom-call.4 | solution.py:29
  225.6 0.3 convolution_bitcast_fusion.4
  225.9 0.2 fusion.16
  226.2 0.2 fusion.12
  226.4 0.4 fusion.14
  226.8 0.4 fusion.19
  227.1 0.2 convolution_multiply_fusion
  227.4 0.1 copy.68
  227.5 11.7 %custom-call.35 = f32[2,64,64]{2,1,0:T(8,128)S(1)} custom-call(f32[2,64,64]{2,1,0:T(8,128)S(1)} %fusion.23), custom_call_target="Cholesky" | custom-call | tf_op jit(solution)/shard_map/vmap(jit(cholesky))/cholesky | solution.py:28
  239.3 0.1 compare_reduce_fusion
  239.4 0.1 select_bitcast_fusion.1
  239.5 9.8 %custom-call.36 = f32[2,1,64,64]{2,3,1,0:T(8,128)S(1)} custom-call(f32[2,1,64,64]{3,2,1,0:T(8,128)S(1)} %select_bitcast_fusion.1), custom_call_target="InvertDiagBlocksLowerTriangular" | custom-call | tf_op jit(solution)/shard_map/vmap()/triangular_solve/custom-call.4 | solution.py:29
  249.3 0.3 fusion.2
  249.6 5.4 %all_gather.11 = bf16[8,128,64]{1,2,0:T(8,128)(2,1)S(1)} all-gather(bf16[2,128,64]{1,2,0:T(8,128)(2,1)S(1)} %fusion.2), channel_id=1, replica_groups=mesh['rows'=8,'groups'=4] {'groups'}, dimensions={0}, use_global_device_ids=true | all-gather | bytes 163840 | tf_op jit(solution)/shard_map/all_gather | solution.py:49
  255.0 8.4 %fusion.1 = bf16[8,4096,64]{1,2,0:T(8,128)(2,1)} fusion(bf16[8,128,64]{1,2,0:T(8,128)(2,1)S(1)} %all_gather.11, bf16[8,4096,128]{2,1,0:T(8,128)(2,1)} %param.11), kind=kOutput, calls=%fused_computation.4 | convolution fusion | flops 538968064 | bytes 12713984 | tf_op jit(solution)/shard_map/srk,skj->srj/dot_general | solution.py:51
  263.4 8.4 %fusion = bf16[8,4096,64]{1,2,0:T(8,128)(2,1)} fusion(bf16[8,128,64]{1,2,0:T(8,128)(2,1)S(1)} %all_gather.11, bf16[8,4096,128]{2,1,0:T(8,128)(2,1)} %param.10), kind=kOutput, calls=%fused_computation.3 | convolution fusion | flops 538968064 | bytes 12713984 | tf_op jit(solution)/shard_map/srk,skj->srj/dot_general | solution.py:50
  271.8 7.8 %pad_maximum_fusion = bf16[8,4096,128]{1,2,0:T(8,128)(2,1)} fusion(bf16[8,4096,64]{1,2,0:T(8,128)(2,1)} %fusion.1, bf16[8,4096,64]{1,2,0:T(8,128)(2,1)} %fusion), kind=kLoop, calls=%fused_computation | loop fusion | flops 16777216 | bytes 16777216 | tf_op jit(solution)/shard_map/concatenate | solution.py:52
  279.6 11.9 %copy.70 = bf16[8,4096,128]{2,1,0:T(8,128)(2,1)} copy(bf16[8,4096,128]{1,2,0:T(8,128)(2,1)} %pad_maximum_fusion) | data formatting | bytes 16777216 | tf_op jit(solution)/shard_map/concatenate | solution.py:52
  (14 shorter events, 0.2 us)
Async XLA Ops:
  6.5 65.6 %copy-start = (s32[8,64]{1,0:T(8,128)S(1)}, s32[8,64]{1,0:T(8,128)}, u32[]{:S(2)}) copy-start(s32[8,64]{1,0:T(8,128)} %param.12) | copy-start | bytes 6148
  6.5 63.8 %all-reduce.3.cloned.1.call-start = ((), (), s32[]{:S(2)}) async-start(), calls=%async_computation.1 | async-start | bytes 3145728
  6.5 8.4 %copy-start.1 = (bf16[8,4096,128]{2,1,0:T(8,128)(2,1)S(1)}, bf16[8,4096,128]{2,1,0:T(8,128)(2,1)}, u32[]{:S(2)}) copy-start(bf16[8,4096,128]{2,1,0:T(8,128)(2,1)} %param.11) | copy-start | bytes 25165828
  20.8 4.0 %copy-start.2 = (u32[32]{0:T(128)S(1)}, u32[32]{0:T(128)}, u32[]{:S(2)}) copy-start(u32[32]{0:T(128)} %constant.93) | copy-start | bytes 388
  24.6 108.1 %all-gather.3.cloned.1.call-start = ((), (), s32[]{:S(2)}) async-start(), calls=%async_computation | async-start | bytes 3538944 | tf_op jit(solution)/shard_map/all_gather | solution.py:43
Sparse Core Ops, SparseCore 0:
  24.7 45.6 all-reduce.2
  72.6 60.0 all-gather.2
